TPU v7x, 128 devices: a whole 4x4x4 slice. The times are simulated.
128 devices in a mesh: blk: 16 (over x, z), order: 8 (over y, core).
Axes of the slice: x: 4, y: 4, z: 4, core: 2. Of those that a mesh axis runs over, the one named last changes fastest.
Arguments:
- field: float32 [16, 1024, 4096], P(None, 'blk', 'order'), may hold values from -6 to 6
- ocean_mask: int32 [1024, 4096], P('blk', 'order'), may hold values from 0 to 1, as said below
- plan: int32 [1024], replicated, may hold values from 0 to 768, as said below
- legendre: bfloat16 [768, 1024, 1024], P('blk', 'order'), may hold values from -0.3125 to 0.3125
Outputs:
- coefficients: float32 [1024, 16, 2, 1024], P('blk', None, None, 'order')
Inputs may be any that keep to these rules, and one draw needn't show every extreme that they name: `ocean_mask`: exactly 256 cycles are all land, at the ends of the cycle order; every other cycle has an ocean point. plan is 768 exactly at the cycles that are all land, and names every slot below 768 once at the other cycles; slot p belongs to index p // 48 of blk; the cycles of one index of blk name at most 4 slots of one index, and in every draw some index of blk names exactly 4 slots of some index.
All inputs are finite; a program needn't handle non-finite values.
Results may differ from a plain program's by a relative error of at most 0.0029.
Values may be sent and summed in bfloat16 or wider, within the bound.
A program may use at most 128 MiB of HBM per device.

v0:
```python
import math
import jax
import jax.numpy as jnp
from jax import lax
from jax.sharding import PartitionSpec as P

NLON = 4096
M = 1024


def twiddle(first, count):
    longitudes = first + jnp.arange(count, dtype=jnp.int32)
    orders = jnp.arange(M, dtype=jnp.int32)
    product = longitudes[:, None] * orders[None, :] % NLON
    angle = product.astype(jnp.float32) * (2.0 * math.pi / NLON)
    scale = 1.0 / math.sqrt(NLON)
    return jnp.stack([jnp.cos(angle) * scale, -jnp.sin(angle) * scale], axis=1)


def transform(values, table):
    return jnp.einsum("frn,ncm->frcm", values, table, precision=lax.Precision.HIGHEST)


def pack_cycles(masked, plan, slot_dev):
    n_blk = lax.axis_size("blk")
    own_index = lax.axis_index("blk")
    cycle_dev = masked.shape[1]
    cap = (cycle_dev + n_blk - 1) // n_blk
    grid = plan.reshape(n_blk, cycle_dev)
    owner = grid // slot_dev
    positions = jnp.arange(cycle_dev, dtype=jnp.int32)
    earlier = positions[None, :] < positions[:, None]
    same_owner = owner[:, :, None] == owner[:, None, :]
    rank = jnp.sum(same_owner & earlier[None], axis=2, dtype=jnp.int32)
    send_pos = owner * cap + rank
    local_pos = lax.dynamic_index_in_dim(send_pos, own_index, 0, keepdims=False)
    buffer_ids = jnp.arange(n_blk * cap, dtype=jnp.int32)
    send_onehot = (buffer_ids[:, None] == local_pos[None, :]).astype(jnp.float32)
    outgoing = jnp.einsum("qr,frn->fqn", send_onehot, masked, precision=lax.Precision.HIGHEST)
    arrived = lax.all_to_all(outgoing, "blk", split_axis=1, concat_axis=1, tiled=True)
    source_pos = (jnp.arange(n_blk, dtype=jnp.int32)[:, None] * cap + rank).reshape(-1)
    mine = (owner == own_index).reshape(-1)
    slot_local = (grid % slot_dev).reshape(-1)
    slot_ids = jnp.arange(slot_dev, dtype=jnp.int32)
    slot_onehot = ((slot_local[None, :] == slot_ids[:, None]) & mine[None, :]).astype(jnp.float32)
    source_onehot = (source_pos[:, None] == buffer_ids[None, :]).astype(jnp.float32)
    receive_map = jnp.dot(slot_onehot, source_onehot, precision=lax.Precision.HIGHEST)
    return jnp.einsum("pq,fqn->fpn", receive_map, arrived, precision=lax.Precision.HIGHEST)


def body(field, ocean_mask, plan, legendre):
    lon_local = field.shape[2]
    slot_dev = legendre.shape[0]
    masked = field * ocean_mask.astype(jnp.float32)[None]
    packed = pack_cycles(masked, plan, slot_dev)
    first = lax.axis_index("order") * lon_local
    terms = transform(packed, twiddle(first, lon_local))
    spectrum = lax.psum_scatter(terms, "order", scatter_dimension=3, tiled=True).astype(
        jnp.bfloat16
    )
    terms = jnp.einsum("pml,fpcm->lfcm", legendre, spectrum, preferred_element_type=jnp.float32)
    coefficients = lax.psum_scatter(terms, "blk", scatter_dimension=0, tiled=True)
    return coefficients


def solution(mesh):
    placed = (P(None, "blk", "order"), P("blk", "order"), P(), P("blk", "order", None))
    return jax.shard_map(
        body, mesh=mesh, in_specs=placed, out_specs=P("blk", None, None, "order"), check_vma=False
    )
```

profile of v0, /device:TPU:1, one launch (start us, length us, event | category | flops | bytes accessed | tf_op | source)
XLA Modules:
  0.0 278.1 jit_solution(17178055627215693072)
XLA Ops:
  6.6 0.7 add_select_fusion.3
  7.3 0.7 fusion.31
  8.0 0.1 and.67
  8.0 0.1 div.20
  8.1 0.9 convert_element_type.26
  9.0 0.5 convert_reduce_fusion
  9.6 3.0 %fusion.18 = f32[16,64,512]{2,1,0:T(8,128)S(1)} fusion(f32[16,64,512]{2,1,0:T(8,128)} %param.4, f32[64,512]{1,0:T(8,128)S(1)} %convert_element_type.26, s32[64]{0:T(128)S(1)} %fusion.33), kind=kOutput, calls=%fused_computation.22 | convolution fusion | flops 403181568 | bytes 4325632 | tf_op jit(solution)/shard_map/qr,frn->fqn/dot_general | solution.py:39
  12.6 2.5 copy.10
  15.1 8.4 %all-to-all-start = ((f32[16,64,512]{2,0,1:T(8,128)}), f32[16,64,512]{2,0,1:T(8,128)S(1)}, u32[]{:S(2)}, u32[]{:S(2)}) async-start(f32[16,64,512]{2,0,1:T(8,128)} %copy.10), calls=%async_computation | async-start | bytes 4194304 | tf_op jit(solution)/shard_map/all_to_all | solution.py:40
  23.5 0.0 reduce-scatter.3.cloned.1.call-start
  23.6 0.1 broadcast_add_fusion
  23.7 0.1 add.77
  23.8 0.3 convolution_bitcast_fusion
  24.1 10.8 %cosine_multiply_fusion = (f32[512,1,1024]{2,0,1:T(8,128)}, f32[512,1,1024]{2,0,1:T(8,128)}) fusion(s32[512]{0:T(512)S(1)} %iota_add_fusion), kind=kLoop, calls=%fused_computation.16 | loop fusion | flops 8912896 | bytes 4196352 | tf_op jit(solution)/shard_map/mul | solution.py:17
  34.8 16.8 %all-to-all-done = f32[16,64,512]{2,0,1:T(8,128)S(1)} async-done(((f32[16,64,512]{2,0,1:T(8,128)}), f32[16,64,512]{2,0,1:T(8,128)S(1)}, u32[]{:S(2)}, u32[]{:S(2)}) %all-to-all-start) | async-done | bytes 2097184 | tf_op jit(solution)/shard_map/all_to_all | solution.py:40
  51.7 0.0 copy-start
  51.7 2.9 %fusion.11 = f32[16,512,48]{1,2,0:T(8,128)S(1)} fusion(f32[48,64,1]{1,0,2:T(8,128)S(1)} %convolution_bitcast_fusion, f32[16,64,512]{2,0,1:T(8,128)S(1)} %all-to-all-done), kind=kOutput, calls=%fused_computation.13 | convolution fusion | flops 301989888 | bytes 3682304 | tf_op jit(solution)/shard_map/pq,fqn->fpn/dot_general | solution.py:48
  54.6 0.0 copy-done
  54.6 13.4 %fusion.5 = f32[16,48,2,1024]{3,1,2,0:T(8,128)} fusion(f32[512,1,1024]{2,0,1:T(8,128)} %get-tuple-element.10, f32[512,1,1024]{2,0,1:T(8,128)S(1)} %copy-done, f32[16,512,48]{1,2,0:T(8,128)S(1)} %fusion.11), kind=kOutput, calls=%fused_computation.4 | convolution fusion | flops 9664724992 | bytes 12058624 | tf_op jit(solution)/shard_map/frn,ncm->frcm/dot_general | solution.py:21
  68.0 0.0 reduce-scatter.3.cloned.1.call-update
  68.0 0.2 reduce-scatter.5.cloned.1.call-start
  68.3 42.5 %reduce-scatter.3.cloned.1.call-done = f32[16,48,2,128]{3,1,2,0:T(8,128)} async-done(((f32[16,48,2,1024]{3,1,2,0:T(8,128)}), f32[16,48,2,128]{3,1,2,0:T(8,128)}) %reduce-scatter.3.cloned.1.call-update) | async-done | bytes 786448 | tf_op jit(solution)/shard_map/reduce_scatter | solution.py:58
  110.8 1.2 convert_element_type.29
  112.0 1.4 copy.12
  113.4 26.5 %fusion.2 = f32[1024,16,2,128]{0,1,2,3:T(8,128)} fusion(bf16[16,48,2,128]{1,0,2,3:T(8,128)(2,1)S(1)} %copy.12, bf16[48,128,1024,1]{2,1,0,3:T(8,128)(2,1)} %bitcast.24), kind=kOutput, calls=%fused_computation.2 | convolution fusion | flops 402653184 | bytes 29753344 | tf_op jit(solution)/shard_map/pml,fpcm->lfcm/dot_general | solution.py:61
  139.9 17.5 %copy.14 = f32[1024,16,2,128]{3,1,2,0:T(8,128)} copy(f32[1024,16,2,128]{0,1,2,3:T(8,128)} %fusion.2) | data formatting | bytes 33554432 | tf_op jit(solution)/shard_map/pml,fpcm->lfcm/transpose | solution.py:61
  157.4 0.0 reduce-scatter.5.cloned.1.call-update
  157.4 111.1 %reduce-scatter.5.cloned.1.call-done = f32[64,16,2,128]{3,1,2,0:T(8,128)} async-done(((f32[1024,16,2,128]{3,1,2,0:T(8,128)}), f32[64,16,2,128]{3,1,2,0:T(8,128)}) %reduce-scatter.5.cloned.1.call-update) | async-done | bytes 1048592 | tf_op jit(solution)/shard_map/reduce_scatter | solution.py:62
  268.5 2.7 copy.15
  (5 shorter events, 0.0 us)
Async XLA Ops:
  15.1 36.6 %all-to-all-start = ((f32[16,64,512]{2,0,1:T(8,128)}), f32[16,64,512]{2,0,1:T(8,128)S(1)}, u32[]{:S(2)}, u32[]{:S(2)}) async-start(f32[16,64,512]{2,0,1:T(8,128)} %copy.10), calls=%async_computation | async-start | bytes 4194304 | tf_op jit(solution)/shard_map/all_to_all | solution.py:40
  23.5 87.2 %reduce-scatter.3.cloned.1.call-start = ((), (), s32[]{:S(2)}) async-start(), calls=%async_computation.3 | async-start | bytes 7077888 | tf_op jit(solution)/shard_map/reduce_scatter | solution.py:58
  51.7 3.0 %copy-start = (f32[512,1,1024]{2,0,1:T(8,128)S(1)}, f32[512,1,1024]{2,0,1:T(8,128)}, u32[]{:S(2)}) copy-start(f32[512,1,1024]{2,0,1:T(8,128)} %get-tuple-element.9) | copy-start | bytes 6291460
  68.0 200.5 %reduce-scatter.5.cloned.1.call-start = ((), (), s32[]{:S(2)}) async-start(), calls=%async_computation.4 | async-start | bytes 17825792 | tf_op jit(solution)/shard_map/reduce_scatter | solution.py:62
Sparse Core Ops, SparseCore 0:
  68.1 42.5 reduce-scatter.2
  157.5 110.9 reduce-scatter.4
where the time goes:
time: 279 us; the launch traced here: 278 us
  waiting for transfers between devices  170 us (61%)
  matrix products  46.1 us (17%)
  local copies, waits for them, and re-layouts  24.4 us (9%)
  other arithmetic  14.9 us (5%)
  between operations  13.5 us (5%)
  starting transfers between devices  8.68 us (3%)
    reduce_scatter x1, waiting for transfers between devices, body(): lax.psum_scatter(terms, 'blk', scatter_dimension=0, tiled=True)  111 us
    reduce_scatter x1, waiting for transfers between devices, body(): lax.psum_scatter(terms, 'order', scatter_dimension=3, tiled=True)  42.5 us
    dot_general x1, matrix products, body(): jnp.einsum('pml,fpcm->lfcm', legendre, spectrum, preferred_element_type=j...  26.5 us
    transpose x1, local copies, waits for them, and re-layouts, body(): jnp.einsum('pml,fpcm->lfcm', legendre, spectrum, preferred_element_type=j...  17.5 us
    all_to_all x1, waiting for transfers between devices, pack_cycles(): lax.all_to_all(outgoing, 'blk', split_axis=1, concat_axis=1, tiled=True)  16.8 us
    dot_general x1, matrix products, transform(): jnp.einsum('frn,ncm->frcm', values, table, precision=lax.Precision.HIGHEST)  13.4 us
    mul x1, other arithmetic, twiddle(): return jnp.stack([jnp.cos(angle) * scale, -jnp.sin(angle) * scale], axis=1)  10.8 us
    all_to_all x1, starting transfers between devices, pack_cycles(): lax.all_to_all(outgoing, 'blk', split_axis=1, concat_axis=1, tiled=True)  8.42 us
  transfers between devices with their start and end apart: 3, of which 3 were waited for; matrix products, arithmetic and copies ran while one was open for 4% of the time, Pallas kernels for 0%

commit v1 on v0

--- a/solution.py
+++ b/solution.py
@@ -3,6 +3,7 @@
 import jax.numpy as jnp
 from jax import lax
 from jax.sharding import PartitionSpec as P
+from jax.lax import all_to_all, axis_size
 
 NLON = 4096
 M = 1024
@@ -22,6 +23,15 @@
 
 
 def pack_cycles(masked, plan, slot_dev):
+
+    def divide_the_bench(u, axis_id, axis_no, row_dim):
+        p_next = axis_size(axis_id)
+        aux = jnp.split(u, p_next, axis=axis_no)
+        res = jnp.stack(aux)
+        d_next = all_to_all(res, axis_id, 0, 0)
+        b_next = jnp.concatenate(d_next, axis=row_dim)
+        return b_next
+
     n_blk = lax.axis_size("blk")
     own_index = lax.axis_index("blk")
     cycle_dev = masked.shape[1]
@@ -37,7 +47,7 @@
     buffer_ids = jnp.arange(n_blk * cap, dtype=jnp.int32)
     send_onehot = (buffer_ids[:, None] == local_pos[None, :]).astype(jnp.float32)
     outgoing = jnp.einsum("qr,frn->fqn", send_onehot, masked, precision=lax.Precision.HIGHEST)
-    arrived = lax.all_to_all(outgoing, "blk", split_axis=1, concat_axis=1, tiled=True)
+    arrived = divide_the_bench(outgoing, "blk", 1, 1)
     source_pos = (jnp.arange(n_blk, dtype=jnp.int32)[:, None] * cap + rank).reshape(-1)
     mine = (owner == own_index).reshape(-1)
     slot_local = (grid % slot_dev).reshape(-1)

time: 279 us -> 287 us (1.029)
  local copies, waits for them, and re-layouts: 24.4 us -> 33.5 us
    unnamed x2 -> x19, local copies, waits for them, and re-layouts: 0.01 us -> 10.2 us
where the time goes in v1:
time: 287 us; the launch traced here: 286 us
  waiting for transfers between devices  170 us (59%)
  matrix products  44.9 us (16%)
  local copies, waits for them, and re-layouts  33.5 us (12%)
  other arithmetic  14.8 us (5%)
  between operations  13.5 us (5%)
  starting transfers between devices  8.9 us (3%)
    reduce_scatter x1, waiting for transfers between devices, body(): lax.psum_scatter(terms, 'blk', scatter_dimension=0, tiled=True)  111 us
    reduce_scatter x1, waiting for transfers between devices, body(): lax.psum_scatter(terms, 'order', scatter_dimension=3, tiled=True)  42.5 us
    dot_general x1, matrix products, body(): jnp.einsum('pml,fpcm->lfcm', legendre, spectrum, preferred_element_type=j...  26.5 us
    transpose x1, local copies, waits for them, and re-layouts, body(): jnp.einsum('pml,fpcm->lfcm', legendre, spectrum, preferred_element_type=j...  17.5 us
    all_to_all x1, waiting for transfers between devices, divide_the_bench(): d_next = all_to_all(res, axis_id, 0, 0)  16.7 us
    dot_general x1, matrix products, transform(): jnp.einsum('frn,ncm->frcm', values, table, precision=lax.Precision.HIGHEST)  12.1 us
    mul x1, other arithmetic, twiddle(): return jnp.stack([jnp.cos(angle) * scale, -jnp.sin(angle) * scale], axis=1)  10.7 us
    unnamed x19, local copies, waits for them, and re-layouts  10.2 us
  transfers between devices with their start and end apart: 3, of which 3 were waited for; matrix products, arithmetic and copies ran while one was open for 4% of the time, Pallas kernels for 0%

profile of v1, /device:TPU:1, one launch (start us, length us, event | category | flops | bytes accessed | tf_op | source)
XLA Modules:
  0.0 285.9 jit_solution(7186310194876344481)
XLA Ops:
  6.6 0.7 add_select_fusion.3
  7.3 0.7 fusion.47
  8.1 0.9 convert_element_type.26
  9.6 3.0 %fusion.18 = f32[16,64,512]{2,1,0:T(8,128)S(1)} fusion(f32[16,64,512]{2,1,0:T(8,128)} %param.4, f32[64,512]{1,0:T(8,128)S(1)} %convert_element_type.26, s32[64]{0:T(128)S(1)} %fusion.49), kind=kOutput, calls=%fused_computation.22 | convolution fusion | flops 403181568 | bytes 4325632 | tf_op jit(solution)/shard_map/qr,frn->fqn/dot_general | solution.py:49
  12.6 0.7 fusion.41
  13.3 0.7 fusion.40
  13.9 0.7 fusion.39
  14.6 0.7 fusion.38
  15.9 0.7 fusion.36
  16.6 0.7 fusion.35
  17.3 0.7 fusion.34
  18.0 0.7 fusion.33
  18.7 0.7 fusion.32
  19.4 0.7 fusion.31
  20.0 0.7 fusion.30
  20.7 0.7 fusion.29
  21.4 0.7 fusion.28
  22.1 0.7 fusion.27
  22.8 0.7 fusion.26
  23.5 8.4 %all-to-all-start = ((f32[16,16,4,512]{3,2,1,0:T(4,128)}), f32[16,16,4,512]{3,2,1,0:T(4,128)S(1)}, u32[]{:S(2)}, u32[]{:S(2)}) async-start(f32[16,16,4,512]{3,2,1,0:T(4,128)} %fusion.26), calls=%async_computation | async-start | bytes 4194304 | tf_op jit(solution)/shard_map/all_to_all | solution.py:31
  32.6 10.7 %cosine_multiply_fusion = (f32[512,1,1024]{2,0,1:T(8,128)}, f32[512,1,1024]{2,0,1:T(8,128)}) fusion(s32[512]{0:T(512)S(1)} %iota_add_fusion), kind=kLoop, calls=%fused_computation.16 | loop fusion | flops 8912896 | bytes 4196352 | tf_op jit(solution)/shard_map/mul | solution.py:18
  43.3 16.7 %all-to-all-done = f32[16,16,4,512]{3,2,1,0:T(4,128)S(1)} async-done(((f32[16,16,4,512]{3,2,1,0:T(4,128)}), f32[16,16,4,512]{3,2,1,0:T(4,128)S(1)}, u32[]{:S(2)}, u32[]{:S(2)}) %all-to-all-start) | async-done | bytes 2097184 | tf_op jit(solution)/shard_map/all_to_all | solution.py:31
  60.0 0.7 copy.16
  60.7 2.9 %fusion.11 = f32[16,512,48]{1,2,0:T(8,128)S(1)} fusion(f32[48,64,1]{1,0,2:T(8,128)S(1)} %convolution_bitcast_fusion, f32[16,64,512]{2,0,1:T(8,128)S(1)} %bitcast.91), kind=kOutput, calls=%fused_computation.13 | convolution fusion | flops 301989888 | bytes 3682304 | tf_op jit(solution)/shard_map/pq,fqn->fpn/dot_general | solution.py:58
  63.7 12.1 %fusion.5 = f32[16,48,2,1024]{3,1,2,0:T(8,128)} fusion(f32[512,1,1024]{2,0,1:T(8,128)S(1)} %copy-done.1, f32[512,1,1024]{2,0,1:T(8,128)S(1)} %copy-done, f32[16,512,48]{1,2,0:T(8,128)S(1)} %fusion.11), kind=kOutput, calls=%fused_computation.4 | convolution fusion | flops 9664724992 | bytes 12058624 | tf_op jit(solution)/shard_map/frn,ncm->frcm/dot_general | solution.py:22
  76.1 42.5 %reduce-scatter.3.cloned.1.call-done = f32[16,48,2,128]{3,1,2,0:T(8,128)} async-done(((f32[16,48,2,1024]{3,1,2,0:T(8,128)}), f32[16,48,2,128]{3,1,2,0:T(8,128)}) %reduce-scatter.3.cloned.1.call-update) | async-done | bytes 786448 | tf_op jit(solution)/shard_map/reduce_scatter | solution.py:68
  118.6 1.2 convert_element_type.29
  119.8 1.4 copy.18
  121.2 26.5 %fusion.2 = f32[1024,16,2,128]{0,1,2,3:T(8,128)} fusion(bf16[16,48,2,128]{1,0,2,3:T(8,128)(2,1)S(1)} %copy.18, bf16[48,128,1024,1]{2,1,0,3:T(8,128)(2,1)} %bitcast.90), kind=kOutput, calls=%fused_computation.2 | convolution fusion | flops 402653184 | bytes 29753344 | tf_op jit(solution)/shard_map/pml,fpcm->lfcm/dot_general | solution.py:71
  147.7 17.5 %copy.20 = f32[1024,16,2,128]{3,1,2,0:T(8,128)} copy(f32[1024,16,2,128]{0,1,2,3:T(8,128)} %fusion.2) | data formatting | bytes 33554432 | tf_op jit(solution)/shard_map/pml,fpcm->lfcm/transpose | solution.py:71
  165.3 111.0 %reduce-scatter.5.cloned.1.call-done = f32[64,16,2,128]{3,1,2,0:T(8,128)} async-done(((f32[1024,16,2,128]{3,1,2,0:T(8,128)}), f32[64,16,2,128]{3,1,2,0:T(8,128)}) %reduce-scatter.5.cloned.1.call-update) | async-done | bytes 1048592 | tf_op jit(solution)/shard_map/reduce_scatter | solution.py:72
  276.3 2.7 copy.21
  (20 shorter events, 2.4 us)
Async XLA Ops:
  23.5 36.6 %all-to-all-start = ((f32[16,16,4,512]{3,2,1,0:T(4,128)}), f32[16,16,4,512]{3,2,1,0:T(4,128)S(1)}, u32[]{:S(2)}, u32[]{:S(2)}) async-start(f32[16,16,4,512]{3,2,1,0:T(4,128)} %fusion.26), calls=%async_computation | async-start | bytes 4194304 | tf_op jit(solution)/shard_map/all_to_all | solution.py:31
  31.9 86.7 %reduce-scatter.3.cloned.1.call-start = ((), (), s32[]{:S(2)}) async-start(), calls=%async_computation.3 | async-start | bytes 7077888 | tf_op jit(solution)/shard_map/reduce_scatter | solution.py:68
  60.0 3.6 %copy-start.1 = (f32[512,1,1024]{2,0,1:T(8,128)S(1)}, f32[512,1,1024]{2,0,1:T(8,128)}, u32[]{:S(2)}) copy-start(f32[512,1,1024]{2,0,1:T(8,128)} %get-tuple-element.10) | copy-start | bytes 6291460
  60.7 3.0 %copy-start = (f32[512,1,1024]{2,0,1:T(8,128)S(1)}, f32[512,1,1024]{2,0,1:T(8,128)}, u32[]{:S(2)}) copy-start(f32[512,1,1024]{2,0,1:T(8,128)} %get-tuple-element.9) | copy-start | bytes 6291460
  75.9 200.5 %reduce-scatter.5.cloned.1.call-start = ((), (), s32[]{:S(2)}) async-start(), calls=%async_computation.4 | async-start | bytes 17825792 | tf_op jit(solution)/shard_map/reduce_scatter | solution.py:72
Sparse Core Ops, SparseCore 0:
  76.0 42.5 reduce-scatter.2
  165.4 110.8 reduce-scatter.4
